TPU v7x, 32 devices: a whole 2x2x4 slice. The times are simulated.
32 devices in a mesh: section: 4 (over z), shard: 8 (over y, x, core).
Axes of the slice: x: 2, y: 2, z: 4, core: 2. Of those that a mesh axis runs over, the one named last changes fastest.
Arguments:
- grad_parts: bfloat16 [4, 8, 256, 8192], P('section', 'shard'), may hold values from -6 to 6
- params: bfloat16 [4, 256, 8192], P('section', 'shard'), may hold values from -6 to 6
- moment_first: float32 [4, 256, 8192], P('section', 'shard'), may hold values from -6 to 6
- moment_second: float32 [4, 256, 8192], P('section', 'shard'), may hold values from 0.5 to 50
- block_layer: int32 [4, 32], P('section', 'shard'), may hold values from 0 to 7, as said below
- block_valid: int32 [4, 32], P('section', 'shard'), may hold values from 0 to 1
- decay: float32 [8], replicated, may hold values from 0.05 to 1
Outputs:
- new_params: bfloat16 [4, 256, 8192], P('section', 'shard')
- new_first: float32 [4, 256, 8192], P('section', 'shard')
- new_second: float32 [4, 256, 8192], P('section', 'shard')
- ratios: float32 [8], replicated
Inputs may be any that keep to these rules, and one draw needn't show every extreme that they name: `block_layer`: in every section the live slots come first. One section has all 32 slots live; each other section has between 16 and 32 live slots, and all sections together have 3 * 32. Over the live slots taken section by section in order, layer ids never fall and every layer has exactly 12 live slots; dead slots hold arbitrary layer ids.
All inputs are finite; a program needn't handle non-finite values.
Results may differ from a plain program's by a relative error of at most 0.008.
Values may be sent and summed in bfloat16 or wider, within the bound.
No kernel may reach another device: no remote copies, remote signals or barrier semaphores. Data moves between devices by JAX's collectives and lax.ppermute only.
A program may use at most 64 MiB of HBM per device.

v0:
```python
import jax
import jax.numpy as jnp
from jax import lax
from jax.experimental import pallas as pl
from jax.experimental.pallas import tpu as pltpu
from jax.sharding import PartitionSpec as P

bias_first = 1.0 - 0.9**10
bias_second = 1.0 - 0.99**10

vmem_bytes = 3 << 19


def bits_of(size):
    return size.bit_length() - 1


def reversed_bits(value, bits):
    return sum(((value >> b) & 1) << (bits - 1 - b) for b in range(bits))


def swapped(size, distance_of):
    return [(i, i ^ distance_of(i)) for i in range(size)]


def after(value, *earlier):
    return lax.optimization_barrier((value, *earlier))[0]


def owner_of(me, r, to_core, bits):
    away = jnp.where(to_core == 0, r, reversed_bits(r, bits))
    return (((me >> 1) ^ away) << 1) | to_core


def partner_rows(parts, me, chosen, rows, bits):
    def copies(me_ref, parts_ref, *refs):
        outs, sems = refs[: len(chosen)], refs[len(chosen)]
        own_index = me_ref[0]
        started = []
        for g, r in enumerate(chosen):
            owner = owner_of(own_index, r, 1 - (own_index & 1), bits)
            source = parts_ref.at[pl.ds(pl.multiple_of(owner * rows, rows), rows)]
            started.append(pltpu.make_async_copy(source, outs[g], sems.at[g]))
        for copy in started:
            copy.start()
        for copy in started:
            copy.wait()

    shape = (rows, parts.shape[1])
    moved = 4 * len(chosen) * shape[0] * shape[1]
    return pl.pallas_call(
        copies,
        out_shape=[pltpu.VMEM(shape, parts.dtype)] * len(chosen),
        in_specs=[
            pl.BlockSpec(memory_space=pltpu.SMEM),
            pl.BlockSpec(memory_space=pl.ANY),
        ],
        out_specs=[pl.BlockSpec(memory_space=pltpu.VMEM)] * len(chosen),
        scratch_shapes=[pltpu.SemaphoreType.DMA((len(chosen),))],
        cost_estimate=pl.CostEstimate(flops=0, transcendentals=0, bytes_accessed=moved),
    )(me.reshape(1), parts)


def scattered_sum(parts, count, rows):
    me = lax.axis_index("shard")
    core = me & 1
    bits = bits_of(count // 2)
    chips = 1 << bits

    def block(r, to_core, held):
        return lax.dynamic_slice_in_dim(held, owner_of(me, r, to_core, bits) * rows, rows, 0)

    def exchanged(away):
        return lax.ppermute(away, "shard", swapped(count, lambda i: 1))

    def core_sum(r):
        return block(r, core, parts).astype(jnp.float32) + partner[r].astype(jnp.float32)

    last = chips - 1
    (away_last,) = partner_rows(parts, me, (last,), rows, bits)
    partner = {last: exchanged(away_last)}
    later = after(parts, away_last)
    in_vmem = min(last, vmem_bytes // (rows * parts.shape[1] * parts.dtype.itemsize))
    chosen = tuple(range(last - 1, last - 1 - in_vmem, -1))
    away = dict(zip(chosen, partner_rows(later, me, chosen, rows, bits)))
    for r in reversed(range(last)):
        partner[r] = exchanged(away[r] if r in away else block(r, 1 - core, later))

    received = {}
    for r in reversed(range(chips)):
        total = core_sum(r)
        arrivals = received.pop(r, [])
        if r == 0:
            for arrival in arrivals[:-1]:
                total = total + arrival.astype(jnp.float32)
            return after(total) + arrivals[-1].astype(jnp.float32)
        for arrival in arrivals:
            total = total + arrival.astype(jnp.float32)
        b = r.bit_length() - 1
        pairs = swapped(
            count, lambda i: (1 << b if i & 1 == 0 else 1 << (bits - 1 - b)) << 1
        )
        sent = total.astype(jnp.bfloat16)
        partner[r - 1] = after(partner[r - 1], sent)
        arrival = lax.ppermute(sent, "shard", pairs)
        received.setdefault(r - (1 << b), []).append(arrival)


def summed_over(value, axis, distance):
    size = lax.axis_size(axis)
    return value + lax.ppermute(value, axis, swapped(size, lambda i: distance))


def step(grad_parts, params, moment_first, moment_second, block_layer, block_valid, decay):
    row_count = params.shape[1]
    n_shard = lax.axis_size("shard")
    n_section = lax.axis_size("section")
    gradient = scattered_sum(grad_parts[0, 0], n_shard, row_count)
    block_rows = row_count // block_layer.shape[1]
    layer_rows = jnp.repeat(block_layer[0], block_rows)
    valid_rows = jnp.repeat(block_valid[0], block_rows) > 0
    layer_ids = jnp.arange(decay.shape[0], dtype=jnp.int32)
    onehot = jnp.where(
        valid_rows[:, None] & (layer_rows[:, None] == layer_ids[None, :]), 1.0, 0.0
    ).astype(jnp.float32)
    weights = params[0].astype(jnp.float32)
    weight_sums = after(jnp.sum(weights * weights, axis=-1))
    row_decay = after(jnp.dot(onehot, decay, precision=lax.Precision.HIGHEST))
    first = 0.9 * moment_first[0] + 0.1 * gradient
    second = 0.99 * moment_second[0] + 0.01 * gradient * gradient
    update = (
        first / bias_first / (jnp.sqrt(second / bias_second) + 1e-06) + row_decay[:, None] * weights
    )
    row_sums = jnp.stack([weight_sums, jnp.sum(update * update, axis=-1)], axis=1)
    partial_value = jnp.dot(onehot.T, row_sums, precision=lax.Precision.HIGHEST)
    late_gradient = after(gradient, partial_value)
    live = valid_rows[:, None]
    first = 0.9 * moment_first[0] + 0.1 * late_gradient
    second = 0.99 * moment_second[0] + 0.01 * late_gradient * late_gradient
    new_first = jnp.where(live, first, moment_first[0])
    new_second = jnp.where(live, second, moment_second[0])
    totals = partial_value
    hops = [("shard", 1 << b) for b in range(bits_of(n_shard))]
    hops += [("section", 1 << b) for b in range(bits_of(n_section))]
    for at, (axis, distance) in enumerate(hops):
        totals = summed_over(totals, axis, distance)
        if at == 1:
            totals, new_first, new_second = lax.optimization_barrier(
                (totals, new_first, new_second)
            )
    ratios = jnp.sqrt(totals[:, 0] / (totals[:, 1] + 1.0))
    row_ratio = jnp.dot(onehot, ratios, precision=lax.Precision.HIGHEST)
    stepped = weights - 0.1 * row_ratio[:, None] * update
    new_params = jnp.where(live, stepped, weights).astype(jnp.bfloat16)
    return (new_params[None], new_first[None], new_second[None], ratios)


def solution(mesh):
    placed = (
        P("section", "shard", None, None),
        P("section", "shard", None),
        P("section", "shard", None),
        P("section", "shard", None),
        P("section", "shard"),
        P("section", "shard"),
        P(),
    )
    return jax.shard_map(
        step,
        mesh=mesh,
        in_specs=placed,
        out_specs=(
            P("section", "shard", None),
            P("section", "shard", None),
            P("section", "shard", None),
            P(),
        ),
        check_vma=False,
    )
```

profile of v0, /device:TPU:0, one launch (start us, length us, event | category | flops | bytes accessed | tf_op | source)
XLA Modules:
  0.0 47.1 jit_solution(6559837154511101337)
XLA Ops:
  0.7 1.1 %shard_map.102 = bf16[32,8192]{1,0:T(8,128)(2,1)S(1)} custom-call(s32[1]{0:T(128)} %bitcast.7.me_ref, bf16[256,8192]{1,0:T(8,128)(2,1)} %bitcast.57), custom_call_target="tpu_custom_call" | custom-call | bytes 1048576 | tf_op jit(solution)/shard_map/pallas_call | solution.py:51
  1.7 0.6 %collective-permute-start.3 = (bf16[32,8192]{1,0:T(8,128)(2,1)S(1)}, bf16[32,8192]{1,0:T(8,128)(2,1)}, u32[]{:S(2)}, u32[]{:S(2)}) collective-permute-start(bf16[32,8192]{1,0:T(8,128)(2,1)S(1)} %shard_map.102), channel_id=1, source_target_pairs={{0,1},{1,0},{2,3},{3,2},{4,5},{5,4},{6,7},{7,6},{8,9},{9,8},{10,11... | collective-permute-start | bytes 1572872 | tf_op jit(solution)/shard_map/ppermute | solution.py:74
  2.3 1.4 %shard_map.103 = (bf16[32,8192]{1,0:T(8,128)(2,1)S(1)}, bf16[32,8192]{1,0:T(8,128)(2,1)S(1)}, bf16[32,8192]{1,0:T(8,128)(2,1)S(1)}) custom-call(s32[1]{0:T(128)} %bitcast.7.me_ref, bf16[256,8192]{1,0:T(8,128)(2,1)} %bitcast.58), custom_call_target="tpu_custom_call" | custom-call | bytes 3145728 | tf_op jit(solution)/shard_map/pallas_call | solution.py:51
  3.7 0.1 collective-permute-start
  3.8 0.5 %collective-permute-start.1 = (bf16[32,8192]{1,0:T(8,128)(2,1)S(1)}, bf16[32,8192]{1,0:T(8,128)(2,1)}, u32[]{:S(2)}, u32[]{:S(2)}) collective-permute-start(bf16[32,8192]{1,0:T(8,128)(2,1)S(1)} %get-tuple-element.17), channel_id=1, source_target_pairs={{0,1},{1,0},{2,3},{3,2},{4,5},{5,4},{6,7},{7,6},{8,9},{9,8},{10,11... | collective-permute-start | bytes 1572872 | tf_op jit(solution)/shard_map/ppermute | solution.py:74
  4.4 0.1 gt.20
  4.7 0.2 convolution_bitcast_fusion.1
  4.9 1.4 %fusion.11 = bf16[32,8192]{1,0:T(8,128)(2,1)S(1)} fusion(bf16[32,8192]{1,0:T(8,128)(2,1)} %collective-permute-done.3, bf16[1,1,256,8192]{3,2,1,0:T(8,128)(2,1)} %param.7, s32[]{:T(128)S(6)} %select_n.41), kind=kLoop, calls=%fused_computation.20 | loop fusion | flops 1048576 | bytes 1572868 | tf_op jit(solution)/shard_map/convert_element_type | solution.py:103
  6.4 3.0 %collective-permute-start.4 = (bf16[32,8192]{1,0:T(8,128)(2,1)S(1)}, bf16[32,8192]{1,0:T(8,128)(2,1)S(1)}, u32[]{:S(2)}, u32[]{:S(2)}) collective-permute-start(bf16[32,8192]{1,0:T(8,128)(2,1)S(1)} %fusion.11), channel_id=1, source_target_pairs={{0,4},{1,3},{2,6},{3,1},{4,0},{5,7},{6,2},{7,5},{8,12},{9,11},{10,... | collective-permute-start | bytes 1572872 | tf_op jit(solution)/shard_map/ppermute | solution.py:105
  9.4 1.3 %fusion.12 = bf16[32,8192]{1,0:T(8,128)(2,1)S(1)} fusion(bf16[32,8192]{1,0:T(8,128)(2,1)} %collective-permute-done.2, bf16[1,1,256,8192]{3,2,1,0:T(8,128)(2,1)} %param.7, s32[]{:T(128)S(6)} %select_n.40), kind=kLoop, calls=%fused_computation.22 | loop fusion | flops 1048576 | bytes 1572868 | tf_op jit(solution)/shard_map/convert_element_type | solution.py:103
  10.7 0.6 %collective-permute-start.5 = (bf16[32,8192]{1,0:T(8,128)(2,1)S(1)}, bf16[32,8192]{1,0:T(8,128)(2,1)S(1)}, u32[]{:S(2)}, u32[]{:S(2)}) collective-permute-start(bf16[32,8192]{1,0:T(8,128)(2,1)S(1)} %fusion.12), channel_id=1, source_target_pairs={{0,4},{1,3},{2,6},{3,1},{4,0},{5,7},{6,2},{7,5},{8,12},{9,11},{10,... | collective-permute-start | bytes 1572872 | tf_op jit(solution)/shard_map/ppermute | solution.py:105
  11.3 5.2 %collective-permute-done.4 = bf16[32,8192]{1,0:T(8,128)(2,1)S(1)} collective-permute-done((bf16[32,8192]{1,0:T(8,128)(2,1)S(1)}, bf16[32,8192]{1,0:T(8,128)(2,1)S(1)}, u32[]{:S(2)}, u32[]{:S(2)}) %collective-permute-start.4) | collective-permute-done | bytes 524320 | tf_op jit(solution)/shard_map/ppermute | solution.py:105
  16.5 1.4 %fusion.14 = bf16[32,8192]{1,0:T(8,128)(2,1)S(1)} fusion(bf16[32,8192]{1,0:T(8,128)(2,1)S(1)} %collective-permute-done.4, bf16[32,8192]{1,0:T(8,128)(2,1)} %collective-permute-done.1, bf16[1,1,256,8192]{3,2,1,0:T(8,128)(2,1)} %param.7, s32[]{:T(128)S(6)} %select_n.38), kind=kLoop, calls=%fused_computation.25 | loop fusion | flops 1572864 | bytes 2097156 | tf_op jit(solution)/shard_map/convert_element_type | solution.py:103
  18.0 2.1 %collective-permute-start.6 = (bf16[32,8192]{1,0:T(8,128)(2,1)S(1)}, bf16[32,8192]{1,0:T(8,128)(2,1)S(1)}, u32[]{:S(2)}, u32[]{:S(2)}) collective-permute-start(bf16[32,8192]{1,0:T(8,128)(2,1)S(1)} %fusion.14), channel_id=1, source_target_pairs={{0,2},{1,5},{2,0},{3,7},{4,6},{5,1},{6,4},{7,3},{8,10},{9,13},{10,... | collective-permute-start | bytes 1572872 | tf_op jit(solution)/shard_map/ppermute | solution.py:105
  20.0 4.1 %collective-permute-done.5 = bf16[32,8192]{1,0:T(8,128)(2,1)S(1)} collective-permute-done((bf16[32,8192]{1,0:T(8,128)(2,1)S(1)}, bf16[32,8192]{1,0:T(8,128)(2,1)S(1)}, u32[]{:S(2)}, u32[]{:S(2)}) %collective-permute-start.5) | collective-permute-done | bytes 524320 | tf_op jit(solution)/shard_map/ppermute | solution.py:105
  24.2 1.4 %fusion.15 = f32[32,8192]{1,0:T(8,128)S(1)} fusion(bf16[32,8192]{1,0:T(8,128)(2,1)S(1)} %collective-permute-done.5, bf16[32,8192]{1,0:T(8,128)(2,1)} %collective-permute-done, bf16[1,1,256,8192]{3,2,1,0:T(8,128)(2,1)} %param.7, s32[]{:T(128)S(6)} %select_n.36), kind=kLoop, calls=%fused_computation.27 | loop fusion | flops 1310720 | bytes 2621444 | tf_op jit(solution)/shard_map/add | solution.py:95
  25.6 1.7 %collective-permute-done.6 = bf16[32,8192]{1,0:T(8,128)(2,1)S(1)} collective-permute-done((bf16[32,8192]{1,0:T(8,128)(2,1)S(1)}, bf16[32,8192]{1,0:T(8,128)(2,1)S(1)}, u32[]{:S(2)}, u32[]{:S(2)}) %collective-permute-start.6) | collective-permute-done | bytes 524320 | tf_op jit(solution)/shard_map/ppermute | solution.py:105
  27.2 1.3 %multiply_reduce_fusion = (f32[32]{0:T(128)S(1)}, f32[32,8192]{1,0:T(8,128)S(1)}, f32[32,8192]{1,0:T(8,128)S(1)}, f32[32]{0:T(128)S(1)}) fusion(bf16[1,32,8192]{2,1,0:T(8,128)(2,1)S(1)} %copy-done.3, f32[32]{0:T(128)S(1)} %convolution_bitcast_fusion.1, f32[1,32,8192]{2,1,0:T(8,128)S(1)} %copy-done.1, f32[1,32,8192]{2,1,0:T(8,128)S(1)} %copy-done.2, ...), kind=kLoop, calls=%fused_computation.31 | loop fusion | flops 5242816 | bytes 6291840 | tf_op jit(solution)/shard_map/reduce_sum | solution.py:134
  28.5 0.2 fusion.18
  28.7 0.4 collective-permute-start.7
  29.1 0.8 %collective-permute-done.7 = f32[8,2]{0,1:T(2,128)S(1)} collective-permute-done((f32[8,2]{0,1:T(2,128)S(1)}, f32[8,2]{0,1:T(2,128)S(1)}, u32[]{:S(2)}, u32[]{:S(2)}) %collective-permute-start.7) | collective-permute-done | bytes 96 | tf_op jit(solution)/shard_map/ppermute | solution.py:111
  29.9 2.0 %collective-permute-start.8 = (f32[8,2]{0,1:T(2,128)S(1)}, f32[8,2]{0,1:T(2,128)S(1)}, u32[]{:S(2)}, u32[]{:S(2)}) collective-permute-start(f32[8,2]{0,1:T(2,128)S(1)} %add.89), channel_id=1, source_target_pairs={{0,2},{1,3},{2,0},{3,1},{4,6},{5,7},{6,4},{7,5},{8,10},{9,11},{10,... | collective-permute-start | bytes 200 | tf_op jit(solution)/shard_map/ppermute | solution.py:111
  31.9 1.7 %fusion.8 = (f32[32,8192]{1,0:T(8,128)}, f32[32,8192]{1,0:T(8,128)}) fusion(f32[32,8192]{1,0:T(8,128)S(1)} %get-tuple-element.22, f32[1,32,8192]{2,1,0:T(8,128)S(1)} %copy-done.1, pred[32]{0:T(512)(128)(4,1)S(1)} %gt.20, f32[1,32,8192]{2,1,0:T(8,128)S(1)} %copy-done.2), kind=kLoop, calls=%fused_computation.16 | loop fusion | flops 2359296 | bytes 5242912 | tf_op jit(solution)/shard_map/jit(_where)/select_n | solution.py:141
  33.7 1.9 %collective-permute-start.9 = (f32[8,2]{0,1:T(2,128)S(1)}, f32[8,2]{0,1:T(2,128)S(1)}, u32[]{:S(2)}, u32[]{:S(2)}) collective-permute-start(f32[8,2]{0,1:T(2,128)S(1)} %add.90), channel_id=1, source_target_pairs={{0,4},{1,5},{2,6},{3,7},{4,0},{5,1},{6,2},{7,3},{8,12},{9,13},{10,... | collective-permute-start | bytes 200 | tf_op jit(solution)/shard_map/ppermute | solution.py:111
  35.5 1.7 %collective-permute-done.9 = f32[8,2]{0,1:T(2,128)S(1)} collective-permute-done((f32[8,2]{0,1:T(2,128)S(1)}, f32[8,2]{0,1:T(2,128)S(1)}, u32[]{:S(2)}, u32[]{:S(2)}) %collective-permute-start.9) | collective-permute-done | bytes 96 | tf_op jit(solution)/shard_map/ppermute | solution.py:111
  37.3 1.9 %collective-permute-start.10 = (f32[8,2]{0,1:T(2,128)S(1)}, f32[8,2]{0,1:T(2,128)S(1)}, u32[]{:S(2)}, u32[]{:S(2)}) collective-permute-start(f32[8,2]{0,1:T(2,128)S(1)} %add.93), channel_id=1, source_target_pairs={{0,8},{8,0},{16,24},{24,16},{1,9},{9,1},{17,25},{25,17},{2,10},{10... | collective-permute-start | bytes 200 | tf_op jit(solution)/shard_map/ppermute | solution.py:111
  39.2 1.7 %collective-permute-done.10 = f32[8,2]{0,1:T(2,128)S(1)} collective-permute-done((f32[8,2]{0,1:T(2,128)S(1)}, f32[8,2]{0,1:T(2,128)S(1)}, u32[]{:S(2)}, u32[]{:S(2)}) %collective-permute-start.10) | collective-permute-done | bytes 96 | tf_op jit(solution)/shard_map/ppermute | solution.py:111
  40.9 2.9 %collective-permute-start.11 = (f32[8,2]{0,1:T(2,128)S(1)}, f32[8,2]{0,1:T(2,128)S(1)}, u32[]{:S(2)}, u32[]{:S(2)}) collective-permute-start(f32[8,2]{0,1:T(2,128)S(1)} %add.94), channel_id=1, source_target_pairs={{0,16},{8,24},{16,0},{24,8},{1,17},{9,25},{17,1},{25,9},{2,18},{10... | collective-permute-start | bytes 200 | tf_op jit(solution)/shard_map/ppermute | solution.py:111
  43.8 1.6 %collective-permute-done.11 = f32[8,2]{0,1:T(2,128)S(1)} collective-permute-done((f32[8,2]{0,1:T(2,128)S(1)}, f32[8,2]{0,1:T(2,128)S(1)}, u32[]{:S(2)}, u32[]{:S(2)}) %collective-permute-start.11) | collective-permute-done | bytes 96 | tf_op jit(solution)/shard_map/ppermute | solution.py:111
  45.3 0.2 fusion
  45.5 0.5 %fusion.51 = f32[8]{0:T(128)} fusion(f32[8,2]{0,1:T(2,128)S(1)} %add.95), kind=kLoop, calls=%fused_computation.66 | loop fusion | flops 16 | bytes 96 | tf_op jit(solution)/shard_map/sqrt | solution.py:151
  46.1 1.0 %fusion.16 = bf16[1,32,8192]{2,1,0:T(8,128)(2,1)} fusion(f32[32,8192]{1,0:T(8,128)S(1)} %get-tuple-element.27, bf16[1,32,8192]{2,1,0:T(8,128)(2,1)S(1)} %copy-done.3, f32[32]{0:T(128)S(1)} %fusion, pred[32]{0:T(512)(128)(4,1)S(1)} %gt.20), kind=kLoop, calls=%fused_computation.33 | loop fusion | flops 1310720 | bytes 2097312 | tf_op jit(solution)/shard_map/broadcast_in_dim | solution.py:155
  (27 shorter events, 0.4 us)
Async XLA Ops:
  0.6 4.1 %copy-start = (f32[8]{0:T(128)S(1)}, f32[8]{0:T(128)}, u32[]{:S(2)}) copy-start(f32[8]{0:T(128)} %param.13) | copy-start | bytes 100
  0.7 3.7 %copy-start.5 = (s32[1,4]{1,0:T(1,128)S(1)}, s32[1,4]{1,0:T(1,128)}, u32[]{:S(2)}) copy-start(s32[1,4]{1,0:T(1,128)} %param.12) | copy-start | bytes 52
  0.7 3.9 %copy-start.4 = (s32[1,4]{1,0:T(1,128)S(1)}, s32[1,4]{1,0:T(1,128)}, u32[]{:S(2)}) copy-start(s32[1,4]{1,0:T(1,128)} %param.11) | copy-start | bytes 52
  1.7 3.2 %collective-permute-start.3 = (bf16[32,8192]{1,0:T(8,128)(2,1)S(1)}, bf16[32,8192]{1,0:T(8,128)(2,1)}, u32[]{:S(2)}, u32[]{:S(2)}) collective-permute-start(bf16[32,8192]{1,0:T(8,128)(2,1)S(1)} %shard_map.102), channel_id=1, source_target_pairs={{0,1},{1,0},{2,3},{3,2},{4,5},{5,4},{6,7},{7,6},{8,9},{9,8},{10,11... | collective-permute-start | bytes 1572872 | tf_op jit(solution)/shard_map/ppermute | solution.py:74
  3.7 23.5 %copy-start.1 = (f32[1,32,8192]{2,1,0:T(8,128)S(1)}, f32[1,32,8192]{2,1,0:T(8,128)}, u32[]{:S(2)}) copy-start(f32[1,32,8192]{2,1,0:T(8,128)} %param.10) | copy-start | bytes 3145732
  3.7 16.3 %collective-permute-start = (bf16[32,8192]{1,0:T(8,128)(2,1)S(1)}, bf16[32,8192]{1,0:T(8,128)(2,1)}, u32[]{:S(2)}, u32[]{:S(2)}) collective-permute-start(bf16[32,8192]{1,0:T(8,128)(2,1)S(1)} %get-tuple-element.16), channel_id=1, source_target_pairs={{0,1},{1,0},{2,3},{3,2},{4,5},{5,4},{6,7},{7,6},{8,9},{9,8},{10,11... | collective-permute-start | bytes 1572872 | tf_op jit(solution)/shard_map/ppermute | solution.py:74
  3.8 7.5 %collective-permute-start.1 = (bf16[32,8192]{1,0:T(8,128)(2,1)S(1)}, bf16[32,8192]{1,0:T(8,128)(2,1)}, u32[]{:S(2)}, u32[]{:S(2)}) collective-permute-start(bf16[32,8192]{1,0:T(8,128)(2,1)S(1)} %get-tuple-element.17), channel_id=1, source_target_pairs={{0,1},{1,0},{2,3},{3,2},{4,5},{5,4},{6,7},{7,6},{8,9},{9,8},{10,11... | collective-permute-start | bytes 1572872 | tf_op jit(solution)/shard_map/ppermute | solution.py:74
  4.3 5.1 %collective-permute-start.2 = (bf16[32,8192]{1,0:T(8,128)(2,1)S(1)}, bf16[32,8192]{1,0:T(8,128)(2,1)}, u32[]{:S(2)}, u32[]{:S(2)}) collective-permute-start(bf16[32,8192]{1,0:T(8,128)(2,1)S(1)} %get-tuple-element.18), channel_id=1, source_target_pairs={{0,1},{1,0},{2,3},{3,2},{4,5},{5,4},{6,7},{7,6},{8,9},{9,8},{10,11... | collective-permute-start | bytes 1572872 | tf_op jit(solution)/shard_map/ppermute | solution.py:74
  4.9 22.3 %copy-start.2 = (f32[1,32,8192]{2,1,0:T(8,128)S(1)}, f32[1,32,8192]{2,1,0:T(8,128)}, u32[]{:S(2)}) copy-start(f32[1,32,8192]{2,1,0:T(8,128)} %param.9) | copy-start | bytes 3145732
  4.9 22.3 %copy-start.3 = (bf16[1,32,8192]{2,1,0:T(8,128)(2,1)S(1)}, bf16[1,32,8192]{2,1,0:T(8,128)(2,1)}, u32[]{:S(2)}) copy-start(bf16[1,32,8192]{2,1,0:T(8,128)(2,1)} %param.8) | copy-start | bytes 1572868
  6.4 10.2 %collective-permute-start.4 = (bf16[32,8192]{1,0:T(8,128)(2,1)S(1)}, bf16[32,8192]{1,0:T(8,128)(2,1)S(1)}, u32[]{:S(2)}, u32[]{:S(2)}) collective-permute-start(bf16[32,8192]{1,0:T(8,128)(2,1)S(1)} %fusion.11), channel_id=1, source_target_pairs={{0,4},{1,3},{2,6},{3,1},{4,0},{5,7},{6,2},{7,5},{8,12},{9,11},{10,... | collective-permute-start | bytes 1572872 | tf_op jit(solution)/shard_map/ppermute | solution.py:105
  10.7 13.5 %collective-permute-start.5 = (bf16[32,8192]{1,0:T(8,128)(2,1)S(1)}, bf16[32,8192]{1,0:T(8,128)(2,1)S(1)}, u32[]{:S(2)}, u32[]{:S(2)}) collective-permute-start(bf16[32,8192]{1,0:T(8,128)(2,1)S(1)} %fusion.12), channel_id=1, source_target_pairs={{0,4},{1,3},{2,6},{3,1},{4,0},{5,7},{6,2},{7,5},{8,12},{9,11},{10,... | collective-permute-start | bytes 1572872 | tf_op jit(solution)/shard_map/ppermute | solution.py:105
  18.0 9.2 %collective-permute-start.6 = (bf16[32,8192]{1,0:T(8,128)(2,1)S(1)}, bf16[32,8192]{1,0:T(8,128)(2,1)S(1)}, u32[]{:S(2)}, u32[]{:S(2)}) collective-permute-start(bf16[32,8192]{1,0:T(8,128)(2,1)S(1)} %fusion.14), channel_id=1, source_target_pairs={{0,2},{1,5},{2,0},{3,7},{4,6},{5,1},{6,4},{7,3},{8,10},{9,13},{10,... | collective-permute-start | bytes 1572872 | tf_op jit(solution)/shard_map/ppermute | solution.py:105
  28.7 1.2 %collective-permute-start.7 = (f32[8,2]{0,1:T(2,128)S(1)}, f32[8,2]{0,1:T(2,128)S(1)}, u32[]{:S(2)}, u32[]{:S(2)}) collective-permute-start(f32[8,2]{0,1:T(2,128)S(1)} %fusion.18), channel_id=1, source_target_pairs={{0,1},{1,0},{2,3},{3,2},{4,5},{5,4},{6,7},{7,6},{8,9},{9,8},{10,11... | collective-permute-start | bytes 200 | tf_op jit(solution)/shard_map/ppermute | solution.py:111
  29.9 3.7 %collective-permute-start.8 = (f32[8,2]{0,1:T(2,128)S(1)}, f32[8,2]{0,1:T(2,128)S(1)}, u32[]{:S(2)}, u32[]{:S(2)}) collective-permute-start(f32[8,2]{0,1:T(2,128)S(1)} %add.89), channel_id=1, source_target_pairs={{0,2},{1,3},{2,0},{3,1},{4,6},{5,7},{6,4},{7,5},{8,10},{9,11},{10,... | collective-permute-start | bytes 200 | tf_op jit(solution)/shard_map/ppermute | solution.py:111
  33.7 3.6 %collective-permute-start.9 = (f32[8,2]{0,1:T(2,128)S(1)}, f32[8,2]{0,1:T(2,128)S(1)}, u32[]{:S(2)}, u32[]{:S(2)}) collective-permute-start(f32[8,2]{0,1:T(2,128)S(1)} %add.90), channel_id=1, source_target_pairs={{0,4},{1,5},{2,6},{3,7},{4,0},{5,1},{6,2},{7,3},{8,12},{9,13},{10,... | collective-permute-start | bytes 200 | tf_op jit(solution)/shard_map/ppermute | solution.py:111
  37.3 3.6 %collective-permute-start.10 = (f32[8,2]{0,1:T(2,128)S(1)}, f32[8,2]{0,1:T(2,128)S(1)}, u32[]{:S(2)}, u32[]{:S(2)}) collective-permute-start(f32[8,2]{0,1:T(2,128)S(1)} %add.93), channel_id=1, source_target_pairs={{0,8},{8,0},{16,24},{24,16},{1,9},{9,1},{17,25},{25,17},{2,10},{10... | collective-permute-start | bytes 200 | tf_op jit(solution)/shard_map/ppermute | solution.py:111
  40.9 4.5 %collective-permute-start.11 = (f32[8,2]{0,1:T(2,128)S(1)}, f32[8,2]{0,1:T(2,128)S(1)}, u32[]{:S(2)}, u32[]{:S(2)}) collective-permute-start(f32[8,2]{0,1:T(2,128)S(1)} %add.94), channel_id=1, source_target_pairs={{0,16},{8,24},{16,0},{24,8},{1,17},{9,25},{17,1},{25,9},{2,18},{10... | collective-permute-start | bytes 200 | tf_op jit(solution)/shard_map/ppermute | solution.py:111
where the time goes:
time: 47.4 us; the launch traced here: 47.1 us
  waiting for transfers between devices  16.8 us (35%)
  starting transfers between devices  15.9 us (34%)
  other arithmetic  10.2 us (22%)
  Pallas kernels  2.45 us (5%)
  between operations  0.73 us (2%)
  matrix products  0.61 us (1%)
    ppermute x3, waiting for transfers between devices, scattered_sum(): arrival = lax.ppermute(sent, 'shard', pairs)  11 us
    ppermute x5, starting transfers between devices, summed_over(): return value + lax.ppermute(value, axis, swapped(size, lambda i: distance))  9.03 us
    ppermute x5, waiting for transfers between devices, summed_over(): return value + lax.ppermute(value, axis, swapped(size, lambda i: distance))  5.84 us
    ppermute x3, starting transfers between devices, scattered_sum(): arrival = lax.ppermute(sent, 'shard', pairs)  5.69 us
    convert_element_type x3, other arithmetic, scattered_sum(): sent = total.astype(jnp.bfloat16)  4.2 us
    pallas_call x2, Pallas kernels, partner_rows(): pl.pallas_call(copies, out_shape=[pltpu.VMEM(shape, parts.dtype)] * len(c...  2.45 us
    select_n x1, other arithmetic, step(): new_second = jnp.where(live, second, moment_second[0])  1.71 us
    add x1, other arithmetic, scattered_sum(): total = total + arrival.astype(jnp.float32)  1.39 us
  transfers between devices with their start and end apart: 12, of which 7 were waited for; matrix products, arithmetic and copies ran while one was open for 17% of the time, Pallas kernels for 3%

commit v1 on v0

--- a/solution.py
+++ b/solution.py
@@ -4,6 +4,7 @@
 from jax.experimental import pallas as pl
 from jax.experimental.pallas import tpu as pltpu
 from jax.sharding import PartitionSpec as P
+
 
 bias_first = 1.0 - 0.9**10
 bias_second = 1.0 - 0.99**10
@@ -83,8 +84,10 @@
     in_vmem = min(last, vmem_bytes // (rows * parts.shape[1] * parts.dtype.itemsize))
     chosen = tuple(range(last - 1, last - 1 - in_vmem, -1))
     away = dict(zip(chosen, partner_rows(later, me, chosen, rows, bits)))
+    lead = core_sum(last).astype(jnp.bfloat16)
     for r in reversed(range(last)):
-        partner[r] = exchanged(away[r] if r in away else block(r, 1 - core, later))
+        waiting = away[r] if r in away else block(r, 1 - core, later)
+        partner[r] = exchanged(after(waiting, lead))
 
     received = {}
     for r in reversed(range(chips)):
@@ -93,7 +96,7 @@
         if r == 0:
             for arrival in arrivals[:-1]:
                 total = total + arrival.astype(jnp.float32)
-            return after(total) + arrivals[-1].astype(jnp.float32)
+            return lead, after(total) + arrivals[-1].astype(jnp.float32)
         for arrival in arrivals:
             total = total + arrival.astype(jnp.float32)
         b = r.bit_length() - 1
@@ -106,16 +109,20 @@
         received.setdefault(r - (1 << b), []).append(arrival)
 
 
-def summed_over(value, axis, distance):
+def summed_over(value, axis, distances):
     size = lax.axis_size(axis)
-    return value + lax.ppermute(value, axis, swapped(size, lambda i: distance))
+    total = value
+    for distance in distances:
+        total = total + lax.ppermute(value, axis, swapped(size, lambda i: distance))
+    return total
 
 
 def step(grad_parts, params, moment_first, moment_second, block_layer, block_valid, decay):
     row_count = params.shape[1]
     n_shard = lax.axis_size("shard")
     n_section = lax.axis_size("section")
-    gradient = scattered_sum(grad_parts[0, 0], n_shard, row_count)
+    lead, gradient = scattered_sum(grad_parts[0, 0], n_shard, row_count)
+    block_layer, block_valid, _ = lax.optimization_barrier((block_layer, block_valid, lead))
     block_rows = row_count // block_layer.shape[1]
     layer_rows = jnp.repeat(block_layer[0], block_rows)
     valid_rows = jnp.repeat(block_valid[0], block_rows) > 0
@@ -133,21 +140,19 @@
     )
     row_sums = jnp.stack([weight_sums, jnp.sum(update * update, axis=-1)], axis=1)
     partial_value = jnp.dot(onehot.T, row_sums, precision=lax.Precision.HIGHEST)
-    late_gradient = after(gradient, partial_value)
+    totals = summed_over(partial_value, "shard", (1,))
+    late_gradient = after(gradient, totals)
     live = valid_rows[:, None]
     first = 0.9 * moment_first[0] + 0.1 * late_gradient
     second = 0.99 * moment_second[0] + 0.01 * late_gradient * late_gradient
     new_first = jnp.where(live, first, moment_first[0])
     new_second = jnp.where(live, second, moment_second[0])
-    totals = partial_value
-    hops = [("shard", 1 << b) for b in range(bits_of(n_shard))]
-    hops += [("section", 1 << b) for b in range(bits_of(n_section))]
-    for at, (axis, distance) in enumerate(hops):
-        totals = summed_over(totals, axis, distance)
-        if at == 1:
-            totals, new_first, new_second = lax.optimization_barrier(
-                (totals, new_first, new_second)
-            )
+    for b in range(1, bits_of(n_shard), 2):
+        pair = (1 << b, 2 << b, 3 << b) if 2 << b < n_shard else (1 << b,)
+        totals = summed_over(totals, "shard", pair)
+    totals, new_first, new_second = lax.optimization_barrier((totals, new_first, new_second))
+    for b in range(bits_of(n_section)):
+        totals = summed_over(totals, "section", (1 << b,))
     ratios = jnp.sqrt(totals[:, 0] / (totals[:, 1] + 1.0))
     row_ratio = jnp.dot(onehot, ratios, precision=lax.Precision.HIGHEST)
     stepped = weights - 0.1 * row_ratio[:, None] * update

time: 47.4 us -> 47.2 us (level)
  starting transfers between devices: 15.9 us -> 15.2 us
  other arithmetic: 10.2 us -> 10.8 us
    convert_element_type x0 -> x1, other arithmetic: none -> 2.18 us  [scattered_sum(): lead = core_sum(last).astype(jnp.bfloat16)]
    convert_element_type x3 -> x2, other arithmetic: 4.2 us -> 2.76 us  [scattered_sum(): sent = total.astype(jnp.bfloat16)]
    ppermute x5 -> x6, starting transfers between devices: 9.03 us -> 7.84 us  [summed_over(): total = total + lax.ppermute(value, axis, swapped(size, lambda i: distance))]
    ppermute x3, waiting for transfers between devices: 11 us -> 9.92 us  [scattered_sum(): arrival = lax.ppermute(sent, 'shard', pairs)]
    ppermute x5 -> x6, waiting for transfers between devices: 5.84 us -> 6.61 us  [summed_over(): total = total + lax.ppermute(value, axis, swapped(size, lambda i: distance))]
  transfers between devices with their start and end apart: 12 -> 13, of which waited for: 7 -> 9; matrix products, arithmetic and copies ran while one was open for 17% -> 13% of each run, Pallas kernels for 3% -> 3%
where the time goes in v1:
time: 47.2 us; the launch traced here: 46.9 us
  waiting for transfers between devices  16.8 us (36%)
  starting transfers between devices  15.2 us (32%)
  other arithmetic  10.8 us (23%)
  Pallas kernels  2.45 us (5%)
  between operations  0.73 us (2%)
  matrix products  0.61 us (1%)
    ppermute x3, waiting for transfers between devices, scattered_sum(): arrival = lax.ppermute(sent, 'shard', pairs)  9.92 us
    ppermute x6, starting transfers between devices, summed_over(): total = total + lax.ppermute(value, axis, swapped(size, lambda i: distance))  7.84 us
    ppermute x6, waiting for transfers between devices, summed_over(): total = total + lax.ppermute(value, axis, swapped(size, lambda i: distance))  6.61 us
    ppermute x3, starting transfers between devices, scattered_sum(): arrival = lax.ppermute(sent, 'shard', pairs)  5.88 us
    convert_element_type x2, other arithmetic, scattered_sum(): sent = total.astype(jnp.bfloat16)  2.76 us
    pallas_call x2, Pallas kernels, partner_rows(): pl.pallas_call(copies, out_shape=[pltpu.VMEM(shape, parts.dtype)] * len(c...  2.45 us
    convert_element_type x1, other arithmetic, scattered_sum(): lead = core_sum(last).astype(jnp.bfloat16)  2.18 us
    select_n x1, other arithmetic, step(): new_second = jnp.where(live, second, moment_second[0])  1.71 us
  transfers between devices with their start and end apart: 13, of which 9 were waited for; matrix products, arithmetic and copies ran while one was open for 13% of the time, Pallas kernels for 3%

profile of v1, /device:TPU:0, one launch (start us, length us, event | category | flops | bytes accessed | tf_op | source)
XLA Modules:
  0.0 46.9 jit_solution(2621354357523679302)
XLA Ops:
  0.7 1.1 %shard_map.102 = bf16[32,8192]{1,0:T(8,128)(2,1)S(1)} custom-call(s32[1]{0:T(128)} %bitcast.1.me_ref, bf16[256,8192]{1,0:T(8,128)(2,1)} %bitcast.57), custom_call_target="tpu_custom_call" | custom-call | bytes 1048576 | tf_op jit(solution)/shard_map/pallas_call | solution.py:52
  1.7 0.6 %collective-permute-start = (bf16[32,8192]{1,0:T(8,128)(2,1)S(1)}, bf16[32,8192]{1,0:T(8,128)(2,1)}, u32[]{:S(2)}, u32[]{:S(2)}) collective-permute-start(bf16[32,8192]{1,0:T(8,128)(2,1)S(1)} %shard_map.102), channel_id=1, source_target_pairs={{0,1},{1,0},{2,3},{3,2},{4,5},{5,4},{6,7},{7,6},{8,9},{9,8},{10,11... | collective-permute-start | bytes 1572872 | tf_op jit(solution)/shard_map/ppermute | solution.py:75
  2.3 1.4 %shard_map.103 = (bf16[32,8192]{1,0:T(8,128)(2,1)S(1)}, bf16[32,8192]{1,0:T(8,128)(2,1)S(1)}, bf16[32,8192]{1,0:T(8,128)(2,1)S(1)}) custom-call(s32[1]{0:T(128)} %bitcast.1.me_ref, bf16[256,8192]{1,0:T(8,128)(2,1)} %bitcast.58), custom_call_target="tpu_custom_call" | custom-call | bytes 3145728 | tf_op jit(solution)/shard_map/pallas_call | solution.py:52
  3.7 0.3 collective-permute-done
  4.0 2.2 %fusion.15 = bf16[32,8192]{1,0:T(8,128)(2,1)} fusion(bf16[32,8192]{1,0:T(8,128)(2,1)} %collective-permute-done, bf16[1,1,256,8192]{3,2,1,0:T(8,128)(2,1)} %param.7, s32[]{:T(128)S(6)} %select_n.37), kind=kLoop, calls=%fused_computation.27 | loop fusion | flops 1048576 | bytes 1572868 | tf_op jit(solution)/shard_map/convert_element_type | solution.py:87
  6.2 0.4 collective-permute-start.3
  6.5 2.6 %collective-permute-start.4 = (bf16[32,8192]{1,0:T(8,128)(2,1)}, bf16[32,8192]{1,0:T(8,128)(2,1)}, u32[]{:S(2)}, u32[]{:S(2)}) collective-permute-start(bf16[32,8192]{1,0:T(8,128)(2,1)} %fusion.15), channel_id=1, source_target_pairs={{0,4},{1,3},{2,6},{3,1},{4,0},{5,7},{6,2},{7,5},{8,12},{9,11},{10,... | collective-permute-start | bytes 1572872 | tf_op jit(solution)/shard_map/ppermute | solution.py:108
  9.5 0.2 convolution_bitcast_fusion.1
  9.8 0.5 collective-permute-start.1
  10.2 1.3 %fusion.11 = bf16[32,8192]{1,0:T(8,128)(2,1)S(1)} fusion(bf16[32,8192]{1,0:T(8,128)(2,1)} %collective-permute-done.3, bf16[1,1,256,8192]{3,2,1,0:T(8,128)(2,1)} %param.7, s32[]{:T(128)S(6)} %select_n.43), kind=kLoop, calls=%fused_computation.20 | loop fusion | flops 1048576 | bytes 1572868 | tf_op jit(solution)/shard_map/convert_element_type | solution.py:106
  11.6 1.2 %collective-permute-start.5 = (bf16[32,8192]{1,0:T(8,128)(2,1)S(1)}, bf16[32,8192]{1,0:T(8,128)(2,1)S(1)}, u32[]{:S(2)}, u32[]{:S(2)}) collective-permute-start(bf16[32,8192]{1,0:T(8,128)(2,1)S(1)} %fusion.11), channel_id=1, source_target_pairs={{0,4},{1,3},{2,6},{3,1},{4,0},{5,7},{6,2},{7,5},{8,12},{9,11},{10,... | collective-permute-start | bytes 1572872 | tf_op jit(solution)/shard_map/ppermute | solution.py:108
  12.7 3.9 %collective-permute-done.4 = bf16[32,8192]{1,0:T(8,128)(2,1)} collective-permute-done((bf16[32,8192]{1,0:T(8,128)(2,1)}, bf16[32,8192]{1,0:T(8,128)(2,1)}, u32[]{:S(2)}, u32[]{:S(2)}) %collective-permute-start.4) | collective-permute-done | bytes 524320 | tf_op jit(solution)/shard_map/ppermute | solution.py:108
  16.6 1.4 %fusion.13 = bf16[32,8192]{1,0:T(8,128)(2,1)S(1)} fusion(bf16[32,8192]{1,0:T(8,128)(2,1)} %collective-permute-done.4, bf16[32,8192]{1,0:T(8,128)(2,1)S(1)} %collective-permute-done.2, bf16[1,1,256,8192]{3,2,1,0:T(8,128)(2,1)} %param.7, s32[]{:T(128)S(6)} %select_n.41), kind=kLoop, calls=%fused_computation.23 | loop fusion | flops 1572864 | bytes 2097156 | tf_op jit(solution)/shard_map/convert_element_type | solution.py:106
  18.1 2.1 %collective-permute-start.6 = (bf16[32,8192]{1,0:T(8,128)(2,1)S(1)}, bf16[32,8192]{1,0:T(8,128)(2,1)S(1)}, u32[]{:S(2)}, u32[]{:S(2)}) collective-permute-start(bf16[32,8192]{1,0:T(8,128)(2,1)S(1)} %fusion.13), channel_id=1, source_target_pairs={{0,2},{1,5},{2,0},{3,7},{4,6},{5,1},{6,4},{7,3},{8,10},{9,13},{10,... | collective-permute-start | bytes 1572872 | tf_op jit(solution)/shard_map/ppermute | solution.py:108
  20.1 3.6 %collective-permute-done.5 = bf16[32,8192]{1,0:T(8,128)(2,1)S(1)} collective-permute-done((bf16[32,8192]{1,0:T(8,128)(2,1)S(1)}, bf16[32,8192]{1,0:T(8,128)(2,1)S(1)}, u32[]{:S(2)}, u32[]{:S(2)}) %collective-permute-start.5) | collective-permute-done | bytes 524320 | tf_op jit(solution)/shard_map/ppermute | solution.py:108
  23.8 1.2 %fusion.14 = f32[32,8192]{1,0:T(8,128)S(1)} fusion(bf16[32,8192]{1,0:T(8,128)(2,1)S(1)} %collective-permute-done.5, bf16[32,8192]{1,0:T(8,128)(2,1)S(1)} %collective-permute-done.1, bf16[1,1,256,8192]{3,2,1,0:T(8,128)(2,1)} %param.7, s32[]{:T(128)S(6)} %select_n.39), kind=kLoop, calls=%fused_computation.25 | loop fusion | flops 1310720 | bytes 2621444 | tf_op jit(solution)/shard_map/add | solution.py:98
  25.0 2.4 %collective-permute-done.6 = bf16[32,8192]{1,0:T(8,128)(2,1)S(1)} collective-permute-done((bf16[32,8192]{1,0:T(8,128)(2,1)S(1)}, bf16[32,8192]{1,0:T(8,128)(2,1)S(1)}, u32[]{:S(2)}, u32[]{:S(2)}) %collective-permute-start.6) | collective-permute-done | bytes 524320 | tf_op jit(solution)/shard_map/ppermute | solution.py:108
  27.4 1.3 %multiply_reduce_fusion = (f32[32]{0:T(128)S(1)}, f32[32,8192]{1,0:T(8,128)S(1)}, f32[32,8192]{1,0:T(8,128)S(1)}, f32[32]{0:T(128)S(1)}) fusion(bf16[1,32,8192]{2,1,0:T(8,128)(2,1)S(1)} %copy-done.3, f32[32]{0:T(128)S(1)} %convolution_bitcast_fusion.1, f32[1,32,8192]{2,1,0:T(8,128)S(1)} %copy-done.1, f32[1,32,8192]{2,1,0:T(8,128)S(1)} %copy-done.2, ...), kind=kLoop, calls=%fused_computation.31 | loop fusion | flops 5242816 | bytes 6291840 | tf_op jit(solution)/shard_map/reduce_sum | solution.py:141
  28.7 0.2 fusion.18
  29.1 1.0 %collective-permute-done.7 = f32[8,2]{0,1:T(2,128)S(1)} collective-permute-done((f32[8,2]{0,1:T(2,128)S(1)}, f32[8,2]{0,1:T(2,128)S(1)}, u32[]{:S(2)}, u32[]{:S(2)}) %collective-permute-start.7) | collective-permute-done | bytes 96 | tf_op jit(solution)/shard_map/ppermute | solution.py:116
  30.1 2.9 %collective-permute-start.10 = (f32[8,2]{0,1:T(2,128)S(1)}, f32[8,2]{0,1:T(2,128)S(1)}, u32[]{:S(2)}, u32[]{:S(2)}) collective-permute-start(f32[8,2]{0,1:T(2,128)S(1)} %add.94), channel_id=1, source_target_pairs={{0,6},{1,7},{2,4},{3,5},{4,2},{5,3},{6,0},{7,1},{8,14},{9,15},{10,... | collective-permute-start | bytes 200 | tf_op jit(solution)/shard_map/ppermute | solution.py:116
  33.0 0.5 %collective-permute-start.9 = (f32[8,2]{0,1:T(2,128)S(1)}, f32[8,2]{0,1:T(2,128)S(1)}, u32[]{:S(2)}, u32[]{:S(2)}) collective-permute-start(f32[8,2]{0,1:T(2,128)S(1)} %add.94), channel_id=1, source_target_pairs={{0,4},{1,5},{2,6},{3,7},{4,0},{5,1},{6,2},{7,3},{8,12},{9,13},{10,... | collective-permute-start | bytes 200 | tf_op jit(solution)/shard_map/ppermute | solution.py:116
  33.6 1.7 %fusion.8 = (f32[32,8192]{1,0:T(8,128)}, f32[32,8192]{1,0:T(8,128)}) fusion(f32[32,8192]{1,0:T(8,128)S(1)} %get-tuple-element.32, f32[1,32,8192]{2,1,0:T(8,128)S(1)} %copy-done.1, pred[32]{0:T(512)(128)(4,1)S(1)} %gt.20, f32[1,32,8192]{2,1,0:T(8,128)S(1)} %copy-done.2), kind=kLoop, calls=%fused_computation.16 | loop fusion | flops 2359296 | bytes 5242912 | tf_op jit(solution)/shard_map/jit(_where)/select_n | solution.py:149
  35.3 1.2 %collective-permute-done.9 = f32[8,2]{0,1:T(2,128)S(1)} collective-permute-done((f32[8,2]{0,1:T(2,128)S(1)}, f32[8,2]{0,1:T(2,128)S(1)}, u32[]{:S(2)}, u32[]{:S(2)}) %collective-permute-start.9) | collective-permute-done | bytes 96 | tf_op jit(solution)/shard_map/ppermute | solution.py:116
  36.5 0.5 %collective-permute-done.8 = f32[8,2]{0,1:T(2,128)S(1)} collective-permute-done((f32[8,2]{0,1:T(2,128)S(1)}, f32[8,2]{0,1:T(2,128)S(1)}, u32[]{:S(2)}, u32[]{:S(2)}) %collective-permute-start.8) | collective-permute-done | bytes 96 | tf_op jit(solution)/shard_map/ppermute | solution.py:116
  37.1 1.6 %collective-permute-start.11 = (f32[8,2]{0,1:T(2,128)S(1)}, f32[8,2]{0,1:T(2,128)S(1)}, u32[]{:S(2)}, u32[]{:S(2)}) collective-permute-start(f32[8,2]{0,1:T(2,128)S(1)} %add_add_fusion), channel_id=1, source_target_pairs={{0,8},{8,0},{16,24},{24,16},{1,9},{9,1},{17,25},{25,17},{2,10},{10... | collective-permute-start | bytes 200 | tf_op jit(solution)/shard_map/ppermute | solution.py:116
  38.6 2.0 %collective-permute-done.11 = f32[8,2]{0,1:T(2,128)S(1)} collective-permute-done((f32[8,2]{0,1:T(2,128)S(1)}, f32[8,2]{0,1:T(2,128)S(1)}, u32[]{:S(2)}, u32[]{:S(2)}) %collective-permute-start.11) | collective-permute-done | bytes 96 | tf_op jit(solution)/shard_map/ppermute | solution.py:116
  40.6 2.6 %collective-permute-start.12 = (f32[8,2]{0,1:T(2,128)S(1)}, f32[8,2]{0,1:T(2,128)S(1)}, u32[]{:S(2)}, u32[]{:S(2)}) collective-permute-start(f32[8,2]{0,1:T(2,128)S(1)} %add.100), channel_id=1, source_target_pairs={{0,16},{8,24},{16,0},{24,8},{1,17},{9,25},{17,1},{25,9},{2,18},{10... | collective-permute-start | bytes 200 | tf_op jit(solution)/shard_map/ppermute | solution.py:116
  43.2 1.9 %collective-permute-done.12 = f32[8,2]{0,1:T(2,128)S(1)} collective-permute-done((f32[8,2]{0,1:T(2,128)S(1)}, f32[8,2]{0,1:T(2,128)S(1)}, u32[]{:S(2)}, u32[]{:S(2)}) %collective-permute-start.12) | collective-permute-done | bytes 96 | tf_op jit(solution)/shard_map/ppermute | solution.py:116
  45.1 0.2 fusion
  45.3 0.5 %fusion.51 = f32[8]{0:T(128)} fusion(f32[8,2]{0,1:T(2,128)S(1)} %add.101), kind=kLoop, calls=%fused_computation.67 | loop fusion | flops 16 | bytes 96 | tf_op jit(solution)/shard_map/sqrt | solution.py:156
  45.9 1.0 %fusion.16 = bf16[1,32,8192]{2,1,0:T(8,128)(2,1)} fusion(f32[32,8192]{1,0:T(8,128)S(1)} %get-tuple-element.37, bf16[1,32,8192]{2,1,0:T(8,128)(2,1)S(1)} %copy-done.3, f32[32]{0:T(128)S(1)} %fusion, pred[32]{0:T(512)(128)(4,1)S(1)} %gt.20), kind=kLoop, calls=%fused_computation.33 | loop fusion | flops 1310720 | bytes 2097312 | tf_op jit(solution)/shard_map/broadcast_in_dim | solution.py:160
  (28 shorter events, 0.8 us)
Async XLA Ops:
  0.6 8.9 %copy-start = (f32[8]{0:T(128)S(1)}, f32[8]{0:T(128)}, u32[]{:S(2)}) copy-start(f32[8]{0:T(128)} %param.13) | copy-start | bytes 100
  0.7 8.5 %copy-start.5 = (s32[1,4]{1,0:T(1,128)S(1)}, s32[1,4]{1,0:T(1,128)}, u32[]{:S(2)}) copy-start(s32[1,4]{1,0:T(1,128)} %param.12) | copy-start | bytes 52
  0.7 8.7 %copy-start.4 = (s32[1,4]{1,0:T(1,128)S(1)}, s32[1,4]{1,0:T(1,128)}, u32[]{:S(2)}) copy-start(s32[1,4]{1,0:T(1,128)} %param.11) | copy-start | bytes 52
  1.7 2.2 %collective-permute-start = (bf16[32,8192]{1,0:T(8,128)(2,1)S(1)}, bf16[32,8192]{1,0:T(8,128)(2,1)}, u32[]{:S(2)}, u32[]{:S(2)}) collective-permute-start(bf16[32,8192]{1,0:T(8,128)(2,1)S(1)} %shard_map.102), channel_id=1, source_target_pairs={{0,1},{1,0},{2,3},{3,2},{4,5},{5,4},{6,7},{7,6},{8,9},{9,8},{10,11... | collective-permute-start | bytes 1572872 | tf_op jit(solution)/shard_map/ppermute | solution.py:75
  3.7 23.7 %copy-start.1 = (f32[1,32,8192]{2,1,0:T(8,128)S(1)}, f32[1,32,8192]{2,1,0:T(8,128)}, u32[]{:S(2)}) copy-start(f32[1,32,8192]{2,1,0:T(8,128)} %param.10) | copy-start | bytes 3145732
  4.0 23.5 %copy-start.3 = (bf16[1,32,8192]{2,1,0:T(8,128)(2,1)S(1)}, bf16[1,32,8192]{2,1,0:T(8,128)(2,1)}, u32[]{:S(2)}) copy-start(bf16[1,32,8192]{2,1,0:T(8,128)(2,1)} %param.8) | copy-start | bytes 1572868
  6.2 4.1 %collective-permute-start.3 = (bf16[32,8192]{1,0:T(8,128)(2,1)S(1)}, bf16[32,8192]{1,0:T(8,128)(2,1)}, u32[]{:S(2)}, u32[]{:S(2)}) collective-permute-start(bf16[32,8192]{1,0:T(8,128)(2,1)S(1)} %get-tuple-element.28), channel_id=1, source_target_pairs={{0,1},{1,0},{2,3},{3,2},{4,5},{5,4},{6,7},{7,6},{8,9},{9,8},{10,11... | collective-permute-start | bytes 1572872 | tf_op jit(solution)/shard_map/ppermute | solution.py:75
  6.5 10.1 %collective-permute-start.4 = (bf16[32,8192]{1,0:T(8,128)(2,1)}, bf16[32,8192]{1,0:T(8,128)(2,1)}, u32[]{:S(2)}, u32[]{:S(2)}) collective-permute-start(bf16[32,8192]{1,0:T(8,128)(2,1)} %fusion.15), channel_id=1, source_target_pairs={{0,4},{1,3},{2,6},{3,1},{4,0},{5,7},{6,2},{7,5},{8,12},{9,11},{10,... | collective-permute-start | bytes 1572872 | tf_op jit(solution)/shard_map/ppermute | solution.py:108
  9.5 17.9 %copy-start.2 = (f32[1,32,8192]{2,1,0:T(8,128)S(1)}, f32[1,32,8192]{2,1,0:T(8,128)}, u32[]{:S(2)}) copy-start(f32[1,32,8192]{2,1,0:T(8,128)} %param.9) | copy-start | bytes 3145732
  9.7 3.0 %collective-permute-start.2 = (bf16[32,8192]{1,0:T(8,128)(2,1)S(1)}, bf16[32,8192]{1,0:T(8,128)(2,1)S(1)}, u32[]{:S(2)}, u32[]{:S(2)}) collective-permute-start(bf16[32,8192]{1,0:T(8,128)(2,1)S(1)} %get-tuple-element.26), channel_id=1, source_target_pairs={{0,1},{1,0},{2,3},{3,2},{4,5},{5,4},{6,7},{7,6},{8,9},{9,8},{10,11... | collective-permute-start | bytes 1572872 | tf_op jit(solution)/shard_map/ppermute | solution.py:75
  9.8 10.4 %collective-permute-start.1 = (bf16[32,8192]{1,0:T(8,128)(2,1)S(1)}, bf16[32,8192]{1,0:T(8,128)(2,1)S(1)}, u32[]{:S(2)}, u32[]{:S(2)}) collective-permute-start(bf16[32,8192]{1,0:T(8,128)(2,1)S(1)} %get-tuple-element.24), channel_id=1, source_target_pairs={{0,1},{1,0},{2,3},{3,2},{4,5},{5,4},{6,7},{7,6},{8,9},{9,8},{10,11... | collective-permute-start | bytes 1572872 | tf_op jit(solution)/shard_map/ppermute | solution.py:75
  11.6 12.2 %collective-permute-start.5 = (bf16[32,8192]{1,0:T(8,128)(2,1)S(1)}, bf16[32,8192]{1,0:T(8,128)(2,1)S(1)}, u32[]{:S(2)}, u32[]{:S(2)}) collective-permute-start(bf16[32,8192]{1,0:T(8,128)(2,1)S(1)} %fusion.11), channel_id=1, source_target_pairs={{0,4},{1,3},{2,6},{3,1},{4,0},{5,7},{6,2},{7,5},{8,12},{9,11},{10,... | collective-permute-start | bytes 1572872 | tf_op jit(solution)/shard_map/ppermute | solution.py:108
  18.1 9.3 %collective-permute-start.6 = (bf16[32,8192]{1,0:T(8,128)(2,1)S(1)}, bf16[32,8192]{1,0:T(8,128)(2,1)S(1)}, u32[]{:S(2)}, u32[]{:S(2)}) collective-permute-start(bf16[32,8192]{1,0:T(8,128)(2,1)S(1)} %fusion.13), channel_id=1, source_target_pairs={{0,2},{1,5},{2,0},{3,7},{4,6},{5,1},{6,4},{7,3},{8,10},{9,13},{10,... | collective-permute-start | bytes 1572872 | tf_op jit(solution)/shard_map/ppermute | solution.py:108
  28.9 1.2 %collective-permute-start.7 = (f32[8,2]{0,1:T(2,128)S(1)}, f32[8,2]{0,1:T(2,128)S(1)}, u32[]{:S(2)}, u32[]{:S(2)}) collective-permute-start(f32[8,2]{0,1:T(2,128)S(1)} %fusion.18), channel_id=1, source_target_pairs={{0,1},{1,0},{2,3},{3,2},{4,5},{5,4},{6,7},{7,6},{8,9},{9,8},{10,11... | collective-permute-start | bytes 200 | tf_op jit(solution)/shard_map/ppermute | solution.py:116
  30.1 5.2 %collective-permute-start.10 = (f32[8,2]{0,1:T(2,128)S(1)}, f32[8,2]{0,1:T(2,128)S(1)}, u32[]{:S(2)}, u32[]{:S(2)}) collective-permute-start(f32[8,2]{0,1:T(2,128)S(1)} %add.94), channel_id=1, source_target_pairs={{0,6},{1,7},{2,4},{3,5},{4,2},{5,3},{6,0},{7,1},{8,14},{9,15},{10,... | collective-permute-start | bytes 200 | tf_op jit(solution)/shard_map/ppermute | solution.py:116
  33.0 3.6 %collective-permute-start.9 = (f32[8,2]{0,1:T(2,128)S(1)}, f32[8,2]{0,1:T(2,128)S(1)}, u32[]{:S(2)}, u32[]{:S(2)}) collective-permute-start(f32[8,2]{0,1:T(2,128)S(1)} %add.94), channel_id=1, source_target_pairs={{0,4},{1,5},{2,6},{3,7},{4,0},{5,1},{6,2},{7,3},{8,12},{9,13},{10,... | collective-permute-start | bytes 200 | tf_op jit(solution)/shard_map/ppermute | solution.py:116
  33.5 3.6 %collective-permute-start.8 = (f32[8,2]{0,1:T(2,128)S(1)}, f32[8,2]{0,1:T(2,128)S(1)}, u32[]{:S(2)}, u32[]{:S(2)}) collective-permute-start(f32[8,2]{0,1:T(2,128)S(1)} %add.94), channel_id=1, source_target_pairs={{0,2},{1,3},{2,0},{3,1},{4,6},{5,7},{6,4},{7,5},{8,10},{9,11},{10,... | collective-permute-start | bytes 200 | tf_op jit(solution)/shard_map/ppermute | solution.py:116
  37.1 3.6 %collective-permute-start.11 = (f32[8,2]{0,1:T(2,128)S(1)}, f32[8,2]{0,1:T(2,128)S(1)}, u32[]{:S(2)}, u32[]{:S(2)}) collective-permute-start(f32[8,2]{0,1:T(2,128)S(1)} %add_add_fusion), channel_id=1, source_target_pairs={{0,8},{8,0},{16,24},{24,16},{1,9},{9,1},{17,25},{25,17},{2,10},{10... | collective-permute-start | bytes 200 | tf_op jit(solution)/shard_map/ppermute | solution.py:116
  40.6 4.5 %collective-permute-start.12 = (f32[8,2]{0,1:T(2,128)S(1)}, f32[8,2]{0,1:T(2,128)S(1)}, u32[]{:S(2)}, u32[]{:S(2)}) collective-permute-start(f32[8,2]{0,1:T(2,128)S(1)} %add.100), channel_id=1, source_target_pairs={{0,16},{8,24},{16,0},{24,8},{1,17},{9,25},{17,1},{25,9},{2,18},{10... | collective-permute-start | bytes 200 | tf_op jit(solution)/shard_map/ppermute | solution.py:116
